TPU v7x, 32 devices: a whole 2x2x4 slice. The times are simulated.
32 devices in a mesh: stream: 4 (over z), patch: 8 (over y, x, core).
Axes of the slice: x: 2, y: 2, z: 4, core: 2. Of those that a mesh axis runs over, the one named last changes fastest.
Arguments:
- tokens: bfloat16 [4, 1024, 1536], P('stream', 'patch'), may hold values from -6 to 6
- query_weight: bfloat16 [1536, 768], P('stream'), may hold values from -0.25 to 0.25
- key_weight: bfloat16 [1536, 768], P('stream'), may hold values from -0.25 to 0.25
- value_weight: bfloat16 [1536, 768], P('stream'), may hold values from -0.15625 to 0.15625
- cache_keys: bfloat16 [4, 6144, 768], P('stream', 'patch'), may hold values from -240 to 240, as said below
- cache_values: bfloat16 [4, 6144, 768], P('stream', 'patch'), may hold values from -6 to 6
- lengths: int32 [4, 8], P('stream', 'patch'), may hold values from 1 to 6, as said below
- assign: int32 [4, 256, 1], P('stream', 'patch'), may hold values from 0 to 7; in each aligned block of 32 rows (0 to 31, 32 to 63, ..., all dimensions but the last counted through in order) at most 8 rows name the same one
Outputs:
- attended: bfloat16 [4, 1024, 768], P('stream', 'patch')
- new_keys: bfloat16 [4, 2048, 768], P('stream', 'patch')
- new_values: bfloat16 [4, 2048, 768], P('stream', 'patch')
Inputs may be any that keep to these rules, and one draw needn't show every extreme that they name: `lengths`: each stream's owners hold whole cache blocks of 128 tokens; in every stream exactly two owners hold 6 blocks and every other owner 1 or 2. `assign`: among the 32 groups of one device no owner is named more than 8 times. `cache_keys`: rows past an owner's length are not part of its cache.
All inputs are finite; a program needn't handle non-finite values.
Results may differ from a plain program's by a relative error of at most 0.015.
The roundings to bfloat16 on the way count: a program that leaves them out, or rounds other values in their place, can miss the bound.
Values may be sent and summed in bfloat16 or wider, within the bound.
No kernel may reach another device: no remote copies, remote signals or barrier semaphores. Data moves between devices by JAX's collectives and lax.ppermute only.
A program may use at most 128 MiB of HBM per device.

v0:
```python
import math
import jax
import jax.numpy as jnp
from jax import lax
from jax.sharding import PartitionSpec as P

HEADS = 6
HD = 128
BLOCK = 128
APP = 4
epsilon = 1e-06
masked_score = -1e30


def body(tokens, query_weight, key_weight, value_weight, cache_keys, cache_values, lengths, assign):
    owners = lax.axis_size("patch")
    span_rows = tokens.shape[1]
    width = HEADS * HD
    floats = tokens[0].astype(jnp.float32)
    normed = (
        floats * lax.rsqrt(jnp.mean(floats * floats, axis=-1, keepdims=True) + epsilon)
    ).astype(jnp.bfloat16)
    gathered = lax.all_gather(normed, "stream", axis=0, tiled=True)
    shard_rows = query_weight.shape[0]
    offset = lax.axis_index("stream") * shard_rows
    columns = lax.dynamic_slice_in_dim(gathered, offset, shard_rows, 1)
    joined = jnp.concatenate((query_weight, key_weight, value_weight), axis=1)
    joined_sum = lax.psum_scatter(
        jnp.dot(columns, joined, preferred_element_type=jnp.float32),
        "stream",
        scatter_dimension=0,
        tiled=True,
    )
    query_sum = joined_sum[:, :width]
    key_sum = joined_sum[:, width : 2 * width]
    value_sum = joined_sum[:, 2 * width :]
    queries = query_sum.astype(jnp.bfloat16)
    keys_new = key_sum.astype(jnp.bfloat16)
    values_new = value_sum.astype(jnp.bfloat16)
    group_count = span_rows // APP
    most_slots = max(2, 2 * group_count // owners)
    owner_ids = assign[0, :, 0]
    positions = jnp.arange(group_count, dtype=jnp.int32)
    earlier = positions[None, :] < positions[:, None]
    matches = owner_ids[:, None] == owner_ids[None, :]
    ranks = jnp.sum(jnp.logical_and(matches, earlier).astype(jnp.int32), axis=1)
    targets = owner_ids * most_slots + ranks
    slot_ids = jnp.arange(owners * most_slots, dtype=jnp.int32)
    select = (targets[None, :] == slot_ids[:, None]).astype(jnp.bfloat16)
    grouped = jnp.concatenate(
        (keys_new.reshape(group_count, APP * width), values_new.reshape(group_count, APP * width)),
        axis=1,
    )
    outgoing = jnp.dot(select, grouped, preferred_element_type=jnp.float32).astype(jnp.bfloat16)
    flags_out = jnp.sum(select.astype(jnp.float32), axis=1).astype(jnp.bfloat16)
    incoming, flags_in = (
        lax.all_to_all(outgoing, "patch", split_axis=0, concat_axis=0, tiled=True),
        lax.all_to_all(flags_out, "patch", split_axis=0, concat_axis=0, tiled=True),
    )
    slot_rows = incoming.shape[0] * APP
    app_keys = incoming[:, : APP * width].reshape(slot_rows, width)
    app_values = incoming[:, APP * width :].reshape(slot_rows, width)
    row_valid = jnp.repeat(flags_in, APP) > 0.5
    all_queries = lax.all_gather(queries, "patch", axis=0, tiled=True).reshape(-1, HEADS, HD)
    scale = 1.0 / math.sqrt(HD)
    cache_k = cache_keys[0]
    cache_v = cache_values[0]
    block_count = lengths[0, 0]

    def fold_block(state, key_rows, value_rows, live):
        best, numer_acc, total_acc = state
        scores = (
            jnp.einsum(
                "thd,khd->thk",
                all_queries,
                key_rows.reshape(-1, HEADS, HD),
                preferred_element_type=jnp.float32,
            )
            * scale
        )
        if live is not None:
            scores = jnp.where(live[None, None, :], scores, masked_score)
        block_top = jnp.max(scores, axis=2)
        weights = jnp.exp(scores - block_top[:, :, None])
        if live is not None:
            weights = jnp.where(live[None, None, :], weights, 0.0)
        weights = weights.astype(jnp.bfloat16)
        part_numer = jnp.einsum(
            "thk,khd->thd",
            weights,
            value_rows.reshape(-1, HEADS, HD),
            preferred_element_type=jnp.float32,
        )
        part_total = jnp.sum(weights.astype(jnp.float32), axis=2)
        merged = jnp.maximum(best, block_top)
        old_scale = jnp.exp(best - merged)
        new_scale = jnp.exp(block_top - merged)
        numer_acc = numer_acc * old_scale[:, :, None] + part_numer * new_scale[:, :, None]
        total_acc = total_acc * old_scale + part_total * new_scale
        return (merged, numer_acc, total_acc)

    query_count = all_queries.shape[0]
    start_state = (
        jnp.full((query_count, HEADS), masked_score, jnp.float32),
        jnp.zeros((query_count, HEADS, HD), jnp.float32),
        jnp.zeros((query_count, HEADS), jnp.float32),
    )
    state = fold_block(start_state, app_keys, app_values, row_valid)

    def per_block(block, state):
        key_rows = lax.dynamic_slice_in_dim(cache_k, block * BLOCK, BLOCK, 0)
        value_rows = lax.dynamic_slice_in_dim(cache_v, block * BLOCK, BLOCK, 0)
        return fold_block(state, key_rows, value_rows, None)

    top_row, numer, total = lax.fori_loop(0, block_count, per_block, state)
    got_numer, got_top, got_total = (
        lax.all_to_all(
            numer.reshape(1, -1, width), "patch", split_axis=1, concat_axis=0, tiled=True
        ),
        lax.all_to_all(top_row[None], "patch", split_axis=1, concat_axis=0, tiled=True),
        lax.all_to_all(total[None], "patch", split_axis=1, concat_axis=0, tiled=True),
    )
    best = jnp.max(got_top, axis=0)
    factor = jnp.exp(got_top - best[None])
    sum_numer = jnp.sum(
        got_numer.reshape(owners, span_rows, HEADS, HD) * factor[:, :, :, None], axis=0
    )
    sum_total = jnp.sum(got_total * factor, axis=0)
    result = sum_numer / sum_total[:, :, None]
    attended = result.reshape(1, span_rows, width).astype(jnp.bfloat16)
    return (attended, app_keys[None], app_values[None])


def solution(mesh):
    placed = (
        P("stream", "patch", None),
        P("stream", None),
        P("stream", None),
        P("stream", None),
        P("stream", "patch", None),
        P("stream", "patch", None),
        P("stream", "patch"),
        P("stream", "patch", None),
    )
    return jax.shard_map(
        body,
        mesh=mesh,
        in_specs=placed,
        out_specs=(
            P("stream", "patch", None),
            P("stream", "patch", None),
            P("stream", "patch", None),
        ),
        check_vma=False,
    )
```

profile of v0, /device:TPU:0, one launch (start us, length us, event | category | flops | bytes accessed | tf_op | source)
XLA Modules:
  0.0 303.4 jit_solution(281291631412131650)
XLA Ops:
  8.4 1.9 fusion.17
  10.3 39.8 %all-gather.3.cloned.1.call-done = bf16[512,1536]{1,0:T(8,128)(2,1)} async-done(((bf16[128,1536]{1,0:T(8,128)(2,1)}), bf16[512,1536]{1,0:T(8,128)(2,1)}) %all-gather.3.cloned.1.call-update) | async-done | bytes 1572880 | tf_op jit(solution)/shard_map/all_gather | solution.py:23
  50.2 5.1 %fusion.10 = f32[512,2304]{1,0:T(8,128)} fusion(bf16[384,768]{1,0:T(8,128)(2,1)} %param.13, bf16[384,768]{1,0:T(8,128)(2,1)} %param.12, bf16[384,768]{1,0:T(8,128)(2,1)} %param.11, bf16[512,1536]{1,0:T(8,128)(2,1)} %all-gather.3.cloned.1.call-done, s32[]{:T(128)S(6)} %select_n.17), kind=kOutput, calls=%fused_computation.25 | convolution fusion | flops 911278080 | bytes 6881284 | tf_op jit(solution)/shard_map/dot_general | solution.py:29
  55.3 84.3 %reduce-scatter.2.cloned.1.call-done = f32[128,2304]{1,0:T(8,128)} async-done(((f32[512,2304]{1,0:T(8,128)}), f32[128,2304]{1,0:T(8,128)}) %reduce-scatter.2.cloned.1.call-update) | async-done | bytes 1179664 | tf_op jit(solution)/shard_map/reduce_scatter | solution.py:28
  139.6 1.3 convert.7
  142.6 3.7 %all-to-all-start = ((bf16[8,8,1]{1,2,0:T(2,128)(2,1)}), bf16[8,8,1]{1,2,0:T(2,128)(2,1)S(1)}, u32[]{:S(2)}, u32[]{:S(2)}) async-start(bf16[8,8,1]{1,2,0:T(2,128)(2,1)} %all_to_all.52), calls=%async_computation | async-start | bytes 8192 | tf_op jit(solution)/shard_map/all_to_all | solution.py:58
  146.6 1.4 fusion.5
  147.9 3.0 all-to-all-done
  150.9 3.5 %all-to-all-start.1 = ((bf16[8,8,6144]{2,1,0:T(8,128)(2,1)}), bf16[8,8,6144]{2,1,0:T(8,128)(2,1)S(1)}, u32[]{:S(2)}, u32[]{:S(2)}) async-start(bf16[8,8,6144]{2,1,0:T(8,128)(2,1)} %fusion.5), calls=%async_computation.2 | async-start | bytes 1572864 | tf_op jit(solution)/shard_map/all_to_all | solution.py:57
  154.5 1.5 copy.109
  155.9 1.4 copy.110
  157.7 13.4 %all-to-all-done.1 = bf16[8,8,6144]{2,1,0:T(8,128)(2,1)S(1)} async-done(((bf16[8,8,6144]{2,1,0:T(8,128)(2,1)}), bf16[8,8,6144]{2,1,0:T(8,128)(2,1)S(1)}, u32[]{:S(2)}, u32[]{:S(2)}) %all-to-all-start.1) | async-done | bytes 786464 | tf_op jit(solution)/shard_map/all_to_all | solution.py:57
  171.7 1.3 reshape_reshape.7
  173.0 1.7 copy.104
  174.7 1.6 copy.111
  177.5 2.1 convert_reduce_fusion.1
  181.1 40.9 %while.14 = (s32[]{:T(128)}, f32[1024,6]{0,1:T(8,128)}, f32[1024,6,128]{0,2,1:T(8,128)S(1)}, f32[1024,6]{0,1:T(8,128)}, s32[]{:T(128)}, /*index=5*/bf16[768,768]...) while((s32[]{:T(128)}, f32[1024,6]{0,1:T(8,128)}, ...), condition=%wide.region_9.10_spmd, body=%wide.region_6.9_spmd.sunk | while | flops 412901376 | bytes 19218712 | solution.py:115
  182.8 2.1 bitcast_reduce_fusion.3
  186.1 1.6 fusion.50
  189.5 2.1 bitcast_reduce_fusion.3
  192.8 1.6 fusion.50
  196.2 2.1 bitcast_reduce_fusion.3
  199.5 1.6 fusion.50
  202.9 2.1 bitcast_reduce_fusion.3
  206.2 1.6 fusion.50
  209.5 2.1 bitcast_reduce_fusion.3
  212.9 1.6 fusion.50
  216.2 2.1 bitcast_reduce_fusion.3
  219.5 1.6 fusion.50
  222.0 1.8 copy.113
  224.3 3.8 %reduce.6 = f32[1024,6]{1,0:T(8,128)} reduce(f32[1024,1,6]{2,1,0:T(1,128)} %bitcast.94, f32[]{:T(128)} %broadcast.73), dimensions={1}, to_apply=%bitcast.56.reduce_sub_computation | reduce | bytes 49156
  228.1 2.0 reshape.145
  230.1 3.9 %all-to-all-start.3 = ((f32[8,1,768]{2,1,0:T(1,128)}), f32[8,1,768]{2,1,0:T(1,128)}, u32[]{:S(2)}, u32[]{:S(2)}) async-start(f32[8,1,768]{2,1,0:T(1,128)} %reshape.145), calls=%async_computation.4 | async-start | bytes 49152 | tf_op jit(solution)/shard_map/all_to_all | solution.py:120
  234.1 1.8 copy.117
  235.8 3.8 %reduce.4 = f32[1024,6]{1,0:T(8,128)} reduce(f32[1024,1,6]{2,1,0:T(1,128)} %bitcast.95, f32[]{:T(128)} %broadcast.73), dimensions={1}, to_apply=%bitcast.54.reduce_sub_computation | reduce | bytes 49156
  239.6 2.0 reshape.143
  241.7 4.1 %all-to-all-start.4 = ((f32[8,1,768]{2,1,0:T(1,128)}), f32[8,1,768]{2,1,0:T(1,128)}, u32[]{:S(2)}, u32[]{:S(2)}) async-start(f32[8,1,768]{2,1,0:T(1,128)} %reshape.143), calls=%async_computation.5 | async-start | bytes 49152 | tf_op jit(solution)/shard_map/all_to_all | solution.py:121
  245.8 5.5 %copy.112 = f32[1,1024,768]{2,0,1:T(1,128)} copy(f32[1,1024,768]{1,2,0:T(8,128)S(1)} %bitcast.82) | data formatting | bytes 6291456 | tf_op jit(solution)/shard_map/reshape | solution.py:118
  251.2 4.2 %all-to-all-start.2 = ((f32[1,1024,768]{2,0,1:T(1,128)}), f32[1,1024,768]{2,0,1:T(1,128)S(1)}, u32[]{:S(2)}, u32[]{:S(2)}) async-start(f32[1,1024,768]{2,0,1:T(1,128)} %copy.112), calls=%async_computation.3 | async-start | bytes 6291456 | tf_op jit(solution)/shard_map/all_to_all | solution.py:117
  255.4 2.0 broadcast_in_dim_reshape.6
  258.4 1.4 reduce.7
  259.8 1.7 reshape.146
  263.9 1.5 reduce.5
  265.3 1.7 reshape.144
  268.3 1.9 mul.117
  270.2 3.6 %copy.116 = f32[1,8,128,768]{3,2,1,0:T(8,128)} copy(f32[1,8,128,768]{2,3,1,0:T(8,128)} %bitcast.88) | data formatting | bytes 6291456 | tf_op jit(solution)/shard_map/mul | solution.py:126
  274.8 18.5 %all-to-all-done.2 = f32[1,1024,768]{2,0,1:T(1,128)S(1)} async-done(((f32[1,1024,768]{2,0,1:T(1,128)}), f32[1,1024,768]{2,0,1:T(1,128)S(1)}, u32[]{:S(2)}, u32[]{:S(2)}) %all-to-all-start.2) | async-done | bytes 3145760 | tf_op jit(solution)/shard_map/all_to_all | solution.py:117
  293.5 1.7 copy-done
  (119 shorter events, 28.6 us)
Async XLA Ops:
  7.2 43.0 %all-gather.3.cloned.1.call-start = ((), (), s32[]{:S(2)}) async-start(), calls=%async_computation.6 | async-start | bytes 1966080 | tf_op jit(solution)/shard_map/all_gather | solution.py:23
  10.3 129.3 %reduce-scatter.2.cloned.1.call-start = ((), (), s32[]{:S(2)}) async-start(), calls=%async_computation.7 | async-start | bytes 5898240 | tf_op jit(solution)/shard_map/reduce_scatter | solution.py:28
  55.2 86.4 %copy-start.10 = (s32[1,32,1]{1,2,0:T(1,128)S(1)}, s32[1,32,1]{1,2,0:T(1,128)}, u32[]{:S(2)}) copy-start(s32[1,32,1]{1,2,0:T(1,128)} %param.17) | copy-start | bytes 388
  55.3 99.2 %copy-start.8 = (bf16[1,768,768]{2,1,0:T(8,128)(2,1)S(1)}, bf16[1,768,768]{2,1,0:T(8,128)(2,1)}, u32[]{:S(2)}) copy-start(bf16[1,768,768]{2,1,0:T(8,128)(2,1)} %param.14) | copy-start | bytes 3538948
  55.3 117.7 %all-gather.5.cloned.1.call-start = ((), (), s32[]{:S(2)}) async-start(), calls=%async_computation.8 | async-start | bytes 1769472 | tf_op jit(solution)/shard_map/all_gather | solution.py:64
  141.6 14.3 %copy-start.9 = (bf16[1,768,768]{2,1,0:T(8,128)(2,1)S(1)}, bf16[1,768,768]{2,1,0:T(8,128)(2,1)}, u32[]{:S(2)}) copy-start(bf16[1,768,768]{2,1,0:T(8,128)(2,1)} %param.15) | copy-start | bytes 3538948
  142.6 8.3 %all-to-all-start = ((bf16[8,8,1]{1,2,0:T(2,128)(2,1)}), bf16[8,8,1]{1,2,0:T(2,128)(2,1)S(1)}, u32[]{:S(2)}, u32[]{:S(2)}) async-start(bf16[8,8,1]{1,2,0:T(2,128)(2,1)} %all_to_all.52), calls=%async_computation | async-start | bytes 8192 | tf_op jit(solution)/shard_map/all_to_all | solution.py:58
  150.9 20.2 %all-to-all-start.1 = ((bf16[8,8,6144]{2,1,0:T(8,128)(2,1)}), bf16[8,8,6144]{2,1,0:T(8,128)(2,1)S(1)}, u32[]{:S(2)}, u32[]{:S(2)}) async-start(bf16[8,8,6144]{2,1,0:T(8,128)(2,1)} %fusion.5), calls=%async_computation.2 | async-start | bytes 1572864 | tf_op jit(solution)/shard_map/all_to_all | solution.py:57
  171.2 1.8 copy-start.1
  177.5 2.7 copy-start.2
  182.8 2.7 copy-start.3
  182.8 2.7 copy-start.5
  185.5 0.6 copy-start.4
  185.5 0.6 copy-start.6
  189.5 2.7 copy-start.3
  189.5 2.7 copy-start.5
  192.2 0.6 copy-start.4
  192.2 0.6 copy-start.6
  196.2 2.7 copy-start.3
  196.2 2.7 copy-start.5
  198.9 0.6 copy-start.4
  198.9 0.6 copy-start.6
  202.8 2.7 copy-start.3
  202.8 2.7 copy-start.5
  205.5 0.6 copy-start.4
  205.6 0.6 copy-start.6
  209.5 2.7 copy-start.3
  209.5 2.7 copy-start.5
  212.2 0.6 copy-start.4
  212.2 0.6 copy-start.6
  216.2 2.7 copy-start.3
  216.2 2.7 copy-start.5
  218.9 0.6 copy-start.4
  218.9 0.6 copy-start.6
  230.1 11.5 %all-to-all-start.3 = ((f32[8,1,768]{2,1,0:T(1,128)}), f32[8,1,768]{2,1,0:T(1,128)}, u32[]{:S(2)}, u32[]{:S(2)}) async-start(f32[8,1,768]{2,1,0:T(1,128)} %reshape.145), calls=%async_computation.4 | async-start | bytes 49152 | tf_op jit(solution)/shard_map/all_to_all | solution.py:120
  241.7 9.6 %all-to-all-start.4 = ((f32[8,1,768]{2,1,0:T(1,128)}), f32[8,1,768]{2,1,0:T(1,128)}, u32[]{:S(2)}, u32[]{:S(2)}) async-start(f32[8,1,768]{2,1,0:T(1,128)} %reshape.143), calls=%async_computation.5 | async-start | bytes 49152 | tf_op jit(solution)/shard_map/all_to_all | solution.py:121
  251.2 42.0 %all-to-all-start.2 = ((f32[1,1024,768]{2,0,1:T(1,128)}), f32[1,1024,768]{2,0,1:T(1,128)S(1)}, u32[]{:S(2)}, u32[]{:S(2)}) async-start(f32[1,1024,768]{2,0,1:T(1,128)} %copy.112), calls=%async_computation.3 | async-start | bytes 6291456 | tf_op jit(solution)/shard_map/all_to_all | solution.py:117
  293.3 1.9 copy-start
  295.2 1.0 copy-start.7
Sparse Core Ops, SparseCore 0:
  10.4 39.7 all-gather.2
  55.4 84.1 reduce-scatter.1
  142.0 29.6 all-gather.4
where the time goes:
time: 305 us; the launch traced here: 303 us
  waiting for transfers between devices  159 us (52%)
  local copies, waits for them, and re-layouts  51.4 us (17%)
  matrix products  30.4 us (10%)
  other arithmetic  23.7 us (8%)
  starting transfers between devices  19.5 us (6%)
  between operations  13.9 us (5%)
  loops' own time  5.28 us (2%)
    reduce_scatter x1, waiting for transfers between devices, body(): lax.psum_scatter(jnp.dot(columns, joined, preferred_element_type=jnp.floa...  84.3 us
    all_gather x1, waiting for transfers between devices, body(): gathered = lax.all_gather(normed, 'stream', axis=0, tiled=True)  39.8 us
    all_to_all x1, waiting for transfers between devices, body(): lax.all_to_all(numer.reshape(1, -1, width), 'patch', split_axis=1, concat...  18.5 us
    dot_general x7, matrix products, fold_block(): jnp.einsum('thd,khd->thk', all_queries, key_rows.reshape(-1, HEADS, HD),...  13.5 us
    all_to_all x1, waiting for transfers between devices, body(): lax.all_to_all(outgoing, 'patch', split_axis=0, concat_axis=0, tiled=True)  13.4 us
    unnamed x23, local copies, waits for them, and re-layouts  13.4 us
    dot_general x7, matrix products, fold_block(): jnp.einsum('thk,khd->thd', weights, value_rows.reshape(-1, HEADS, HD), pr...  10.5 us
    unnamed x2, other arithmetic  7.58 us
  transfers between devices with their start and end apart: 8, of which 5 were waited for; matrix products, arithmetic and copies ran while one was open for 13% of the time, Pallas kernels for 0%

commit v1 on v0

--- a/solution.py
+++ b/solution.py
@@ -20,7 +20,14 @@
     normed = (
         floats * lax.rsqrt(jnp.mean(floats * floats, axis=-1, keepdims=True) + epsilon)
     ).astype(jnp.bfloat16)
-    gathered = lax.all_gather(normed, "stream", axis=0, tiled=True)
+    ring = [normed]
+    for hop in range(3):
+        ring.append(lax.ppermute(ring[-1], "stream", [(dev, (dev + 1) % 4) for dev in range(4)]))
+    gathered = jnp.roll(
+        jnp.concatenate(ring[::-1], axis=0),
+        (lax.axis_index("stream") + 1) * ring[0].shape[0],
+        axis=0,
+    )
     shard_rows = query_weight.shape[0]
     offset = lax.axis_index("stream") * shard_rows
     columns = lax.dynamic_slice_in_dim(gathered, offset, shard_rows, 1)

time: 305 us -> 300 us (0.984)
  waiting for transfers between devices: 159 us -> 153 us
  starting transfers between devices: 19.5 us -> 22.6 us
    all_gather x1 -> x0, waiting for transfers between devices: 39.8 us -> none  [body(): gathered = lax.all_gather(normed, 'stream', axis=0, tiled=True)]
    ppermute x0 -> x3, waiting for transfers between devices: none -> 34.4 us  [body(): lax.ppermute(ring[-1], 'stream', [(dev, (dev + 1) % 4) for dev in range(4)])]
    ppermute x0 -> x3, starting transfers between devices: none -> 3.11 us  [body(): lax.ppermute(ring[-1], 'stream', [(dev, (dev + 1) % 4) for dev in range(4)])]
    unnamed x23 -> x37, local copies, waits for them, and re-layouts: 13.4 us -> 13.5 us
    unnamed x2 -> x3, other arithmetic: 7.58 us -> 7.71 us
  transfers between devices with their start and end apart: 8 -> 10, of which waited for: 5 -> 7; matrix products, arithmetic and copies ran while one was open for 13% -> 13% of each run, Pallas kernels for 0% -> 0%
where the time goes in v1:
time: 300 us; the launch traced here: 299 us
  waiting for transfers between devices  153 us (51%)
  local copies, waits for them, and re-layouts  51.6 us (17%)
  matrix products  28.9 us (10%)
  other arithmetic  23.3 us (8%)
  starting transfers between devices  22.6 us (8%)
  between operations  14.3 us (5%)
  loops' own time  5.28 us (2%)
    reduce_scatter x1, waiting for transfers between devices, body(): lax.psum_scatter(jnp.dot(columns, joined, preferred_element_type=jnp.floa...  83.2 us
    ppermute x3, waiting for transfers between devices, body(): lax.ppermute(ring[-1], 'stream', [(dev, (dev + 1) % 4) for dev in range(4)])  34.4 us
    all_to_all x1, waiting for transfers between devices, body(): lax.all_to_all(numer.reshape(1, -1, width), 'patch', split_axis=1, concat...  18.5 us
    unnamed x37, local copies, waits for them, and re-layouts  13.5 us
    dot_general x7, matrix products, fold_block(): jnp.einsum('thd,khd->thk', all_queries, key_rows.reshape(-1, HEADS, HD),...  13.5 us
    all_to_all x1, waiting for transfers between devices, body(): lax.all_to_all(outgoing, 'patch', split_axis=0, concat_axis=0, tiled=True)  13.4 us
    dot_general x7, matrix products, fold_block(): jnp.einsum('thk,khd->thd', weights, value_rows.reshape(-1, HEADS, HD), pr...  10.5 us
    unnamed x3, other arithmetic  7.71 us
  transfers between devices with their start and end apart: 10, of which 7 were waited for; matrix products, arithmetic and copies ran while one was open for 13% of the time, Pallas kernels for 0%

profile of v1, /device:TPU:0, one launch (start us, length us, event | category | flops | bytes accessed | tf_op | source)
XLA Modules:
  0.0 298.6 jit_solution(14723156463012924718)
XLA Ops:
  9.6 3.1 %collective-permute-start = (bf16[128,1536]{1,0:T(8,128)(2,1)S(1)}, bf16[128,1536]{1,0:T(8,128)(2,1)S(1)}, u32[]{:S(2)}, u32[]{:S(2)}) collective-permute-start(bf16[128,1536]{1,0:T(8,128)(2,1)S(1)} %fusion.17), channel_id=1, source_target_pairs={{0,8},{8,16},{16,24},{24,0},{1,9},{9,17},{17,25},{25,1},{2,10},{10... | collective-permute-start | bytes 1179656 | tf_op jit(solution)/shard_map/ppermute | solution.py:25
  12.7 11.1 %collective-permute-done = bf16[128,1536]{1,0:T(8,128)(2,1)S(1)} collective-permute-done((bf16[128,1536]{1,0:T(8,128)(2,1)S(1)}, bf16[128,1536]{1,0:T(8,128)(2,1)S(1)}, u32[]{:S(2)}, u32[]{:S(2)}) %collective-permute-start) | collective-permute-done | bytes 393248 | tf_op jit(solution)/shard_map/ppermute | solution.py:25
  23.8 12.1 %collective-permute-done.1 = bf16[128,1536]{1,0:T(8,128)(2,1)S(1)} collective-permute-done((bf16[128,1536]{1,0:T(8,128)(2,1)S(1)}, bf16[128,1536]{1,0:T(8,128)(2,1)S(1)}, u32[]{:S(2)}, u32[]{:S(2)}) %collective-permute-start.1) | collective-permute-done | bytes 393248 | tf_op jit(solution)/shard_map/ppermute | solution.py:25
  35.9 11.2 %collective-permute-done.2 = bf16[128,1536]{1,0:T(8,128)(2,1)S(1)} collective-permute-done((bf16[128,1536]{1,0:T(8,128)(2,1)S(1)}, bf16[128,1536]{1,0:T(8,128)(2,1)S(1)}, u32[]{:S(2)}, u32[]{:S(2)}) %collective-permute-start.2) | collective-permute-done | bytes 393248 | tf_op jit(solution)/shard_map/ppermute | solution.py:25
  47.6 3.6 %fusion.10 = f32[512,2304]{1,0:T(8,128)} fusion(bf16[384,768]{1,0:T(8,128)(2,1)S(1)} %copy-done.11, bf16[384,768]{1,0:T(8,128)(2,1)S(1)} %copy-done.12, bf16[384,768]{1,0:T(8,128)(2,1)S(1)} %copy-done.13, bf16[1024,1536]{1,0:T(8,128)(2,1)S(1)} %constant_dynamic-update-slice_fusion, s32[]{:T(128)S(6)} %select_n.36, s32[]{:T(128)S(6)} %select_n.38), kind=kOutput, calls=%fused_computation.25 | convolution fusion | flops 911278080 | bytes 6881288 | tf_op jit(solution)/shard_map/dot_general | solution.py:36
  51.3 83.2 %reduce-scatter.2.cloned.1.call-done = f32[128,2304]{1,0:T(8,128)} async-done(((f32[512,2304]{1,0:T(8,128)}), f32[128,2304]{1,0:T(8,128)}) %reduce-scatter.2.cloned.1.call-update) | async-done | bytes 1179664 | tf_op jit(solution)/shard_map/reduce_scatter | solution.py:35
  137.5 3.7 %all-to-all-start = ((bf16[8,8,1]{1,2,0:T(2,128)(2,1)}), bf16[8,8,1]{1,2,0:T(2,128)(2,1)S(1)}, u32[]{:S(2)}, u32[]{:S(2)}) async-start(bf16[8,8,1]{1,2,0:T(2,128)(2,1)} %all_to_all.52), calls=%async_computation | async-start | bytes 8192 | tf_op jit(solution)/shard_map/all_to_all | solution.py:65
  141.5 1.4 fusion.5
  142.8 3.0 all-to-all-done
  145.8 3.5 %all-to-all-start.1 = ((bf16[8,8,6144]{2,1,0:T(8,128)(2,1)}), bf16[8,8,6144]{2,1,0:T(8,128)(2,1)S(1)}, u32[]{:S(2)}, u32[]{:S(2)}) async-start(bf16[8,8,6144]{2,1,0:T(8,128)(2,1)} %fusion.5), calls=%async_computation.2 | async-start | bytes 1572864 | tf_op jit(solution)/shard_map/all_to_all | solution.py:64
  149.4 1.5 copy.109
  150.8 1.4 copy.110
  152.6 13.4 %all-to-all-done.1 = bf16[8,8,6144]{2,1,0:T(8,128)(2,1)S(1)} async-done(((bf16[8,8,6144]{2,1,0:T(8,128)(2,1)}), bf16[8,8,6144]{2,1,0:T(8,128)(2,1)S(1)}, u32[]{:S(2)}, u32[]{:S(2)}) %all-to-all-start.1) | async-done | bytes 786464 | tf_op jit(solution)/shard_map/all_to_all | solution.py:64
  167.9 1.7 copy.104
  169.6 1.6 copy.111
  172.4 2.1 convert_reduce_fusion.1
  176.0 40.9 %while.14 = (s32[]{:T(128)}, f32[1024,6]{0,1:T(8,128)}, f32[1024,6,128]{0,2,1:T(8,128)S(1)}, f32[1024,6]{0,1:T(8,128)}, s32[]{:T(128)}, /*index=5*/bf16[768,768]...) while((s32[]{:T(128)}, f32[1024,6]{0,1:T(8,128)}, ...), condition=%wide.region_9.10_spmd, body=%wide.region_6.9_spmd.sunk | while | flops 412901376 | bytes 19218712 | solution.py:122
  177.7 2.1 bitcast_reduce_fusion.3
  181.0 1.6 fusion.49
  184.4 2.1 bitcast_reduce_fusion.3
  187.7 1.6 fusion.49
  191.1 2.1 bitcast_reduce_fusion.3
  194.4 1.6 fusion.49
  197.8 2.1 bitcast_reduce_fusion.3
  201.1 1.6 fusion.49
  204.4 2.1 bitcast_reduce_fusion.3
  207.7 1.6 fusion.49
  211.1 2.1 bitcast_reduce_fusion.3
  214.4 1.6 fusion.49
  216.9 1.8 copy.113
  219.2 3.8 %reduce.6 = f32[1024,6]{1,0:T(8,128)} reduce(f32[1024,1,6]{2,1,0:T(1,128)} %bitcast.98, f32[]{:T(128)} %broadcast.74), dimensions={1}, to_apply=%bitcast.56.reduce_sub_computation | reduce | bytes 49156
  223.0 2.0 reshape.145
  225.0 3.9 %all-to-all-start.3 = ((f32[8,1,768]{2,1,0:T(1,128)}), f32[8,1,768]{2,1,0:T(1,128)}, u32[]{:S(2)}, u32[]{:S(2)}) async-start(f32[8,1,768]{2,1,0:T(1,128)} %reshape.145), calls=%async_computation.4 | async-start | bytes 49152 | tf_op jit(solution)/shard_map/all_to_all | solution.py:127
  229.0 1.8 copy.117
  230.7 3.8 %reduce.4 = f32[1024,6]{1,0:T(8,128)} reduce(f32[1024,1,6]{2,1,0:T(1,128)} %bitcast.99, f32[]{:T(128)} %broadcast.74), dimensions={1}, to_apply=%bitcast.54.reduce_sub_computation | reduce | bytes 49156
  234.5 2.0 reshape.143
  236.6 4.1 %all-to-all-start.4 = ((f32[8,1,768]{2,1,0:T(1,128)}), f32[8,1,768]{2,1,0:T(1,128)}, u32[]{:S(2)}, u32[]{:S(2)}) async-start(f32[8,1,768]{2,1,0:T(1,128)} %reshape.143), calls=%async_computation.5 | async-start | bytes 49152 | tf_op jit(solution)/shard_map/all_to_all | solution.py:128
  240.7 5.5 %copy.112 = f32[1,1024,768]{2,0,1:T(1,128)} copy(f32[1,1024,768]{1,2,0:T(8,128)S(1)} %bitcast.86) | data formatting | bytes 6291456 | tf_op jit(solution)/shard_map/reshape | solution.py:125
  246.1 4.2 %all-to-all-start.2 = ((f32[1,1024,768]{2,0,1:T(1,128)}), f32[1,1024,768]{2,0,1:T(1,128)S(1)}, u32[]{:S(2)}, u32[]{:S(2)}) async-start(f32[1,1024,768]{2,0,1:T(1,128)} %copy.112), calls=%async_computation.3 | async-start | bytes 6291456 | tf_op jit(solution)/shard_map/all_to_all | solution.py:124
  250.3 2.0 broadcast_in_dim_reshape.6
  253.3 1.4 reduce.7
  254.7 1.7 reshape.146
  258.8 1.5 reduce.5
  260.2 1.7 reshape.144
  263.2 1.9 mul.121
  265.1 3.6 %copy.116 = f32[1,8,128,768]{3,2,1,0:T(8,128)} copy(f32[1,8,128,768]{2,3,1,0:T(8,128)} %bitcast.92) | data formatting | bytes 6291456 | tf_op jit(solution)/shard_map/mul | solution.py:133
  269.6 18.5 %all-to-all-done.2 = f32[1,1024,768]{2,0,1:T(1,128)S(1)} async-done(((f32[1,1024,768]{2,0,1:T(1,128)}), f32[1,1024,768]{2,0,1:T(1,128)S(1)}, u32[]{:S(2)}, u32[]{:S(2)}) %all-to-all-start.2) | async-done | bytes 3145760 | tf_op jit(solution)/shard_map/all_to_all | solution.py:124
  288.4 1.7 copy-done
  (138 shorter events, 32.8 us)
Async XLA Ops:
  7.2 40.1 %copy-start.1 = (bf16[1,128,1536]{2,1,0:T(8,128)(2,1)S(1)}, bf16[1,128,1536]{2,1,0:T(8,128)(2,1)}, u32[]{:S(2)}) copy-start(bf16[1,128,1536]{2,1,0:T(8,128)(2,1)} %param.10) | copy-start | bytes 1179652
  7.2 127.3 %reduce-scatter.2.cloned.1.call-start = ((), (), s32[]{:S(2)}) async-start(), calls=%async_computation.6 | async-start | bytes 5898240 | tf_op jit(solution)/shard_map/reduce_scatter | solution.py:35
  9.6 14.2 %collective-permute-start = (bf16[128,1536]{1,0:T(8,128)(2,1)S(1)}, bf16[128,1536]{1,0:T(8,128)(2,1)S(1)}, u32[]{:S(2)}, u32[]{:S(2)}) collective-permute-start(bf16[128,1536]{1,0:T(8,128)(2,1)S(1)} %fusion.17), channel_id=1, source_target_pairs={{0,8},{8,16},{16,24},{24,0},{1,9},{9,17},{17,25},{25,1},{2,10},{10... | collective-permute-start | bytes 1179656 | tf_op jit(solution)/shard_map/ppermute | solution.py:25
  23.8 12.1 %collective-permute-start.1 = (bf16[128,1536]{1,0:T(8,128)(2,1)S(1)}, bf16[128,1536]{1,0:T(8,128)(2,1)S(1)}, u32[]{:S(2)}, u32[]{:S(2)}) collective-permute-start(bf16[128,1536]{1,0:T(8,128)(2,1)S(1)} %collective-permute-done), channel_id=1, source_target_pairs={{0,8},{8,16},{16,24},{24,0},{1,9},{9,17},{17,25},{25,1},{2,10},{10... | collective-permute-start | bytes 1179656 | tf_op jit(solution)/shard_map/ppermute | solution.py:25
  35.9 11.2 %collective-permute-start.2 = (bf16[128,1536]{1,0:T(8,128)(2,1)S(1)}, bf16[128,1536]{1,0:T(8,128)(2,1)S(1)}, u32[]{:S(2)}, u32[]{:S(2)}) collective-permute-start(bf16[128,1536]{1,0:T(8,128)(2,1)S(1)} %collective-permute-done.1), channel_id=1, source_target_pairs={{0,8},{8,16},{16,24},{24,0},{1,9},{9,17},{17,25},{25,1},{2,10},{10... | collective-permute-start | bytes 1179656 | tf_op jit(solution)/shard_map/ppermute | solution.py:25
  35.9 11.7 %copy-start.11 = (bf16[384,768]{1,0:T(8,128)(2,1)S(1)}, bf16[384,768]{1,0:T(8,128)(2,1)}, u32[]{:S(2)}) copy-start(bf16[384,768]{1,0:T(8,128)(2,1)} %param.13) | copy-start | bytes 1769476
  35.9 11.7 %copy-start.12 = (bf16[384,768]{1,0:T(8,128)(2,1)S(1)}, bf16[384,768]{1,0:T(8,128)(2,1)}, u32[]{:S(2)}) copy-start(bf16[384,768]{1,0:T(8,128)(2,1)} %param.12) | copy-start | bytes 1769476
  35.9 11.7 %copy-start.13 = (bf16[384,768]{1,0:T(8,128)(2,1)S(1)}, bf16[384,768]{1,0:T(8,128)(2,1)}, u32[]{:S(2)}) copy-start(bf16[384,768]{1,0:T(8,128)(2,1)} %param.11) | copy-start | bytes 1769476
  51.2 85.3 %copy-start.14 = (s32[1,32,1]{1,2,0:T(1,128)S(1)}, s32[1,32,1]{1,2,0:T(1,128)}, u32[]{:S(2)}) copy-start(s32[1,32,1]{1,2,0:T(1,128)} %param.17) | copy-start | bytes 388
  51.3 98.1 %copy-start.9 = (bf16[1,768,768]{2,1,0:T(8,128)(2,1)S(1)}, bf16[1,768,768]{2,1,0:T(8,128)(2,1)}, u32[]{:S(2)}) copy-start(bf16[1,768,768]{2,1,0:T(8,128)(2,1)} %param.14) | copy-start | bytes 3538948
  51.3 116.6 %all-gather.2.cloned.1.call-start = ((), (), s32[]{:S(2)}) async-start(), calls=%async_computation.7 | async-start | bytes 1769472 | tf_op jit(solution)/shard_map/all_gather | solution.py:71
  136.5 14.3 %copy-start.10 = (bf16[1,768,768]{2,1,0:T(8,128)(2,1)S(1)}, bf16[1,768,768]{2,1,0:T(8,128)(2,1)}, u32[]{:S(2)}) copy-start(bf16[1,768,768]{2,1,0:T(8,128)(2,1)} %param.15) | copy-start | bytes 3538948
  137.5 8.3 %all-to-all-start = ((bf16[8,8,1]{1,2,0:T(2,128)(2,1)}), bf16[8,8,1]{1,2,0:T(2,128)(2,1)S(1)}, u32[]{:S(2)}, u32[]{:S(2)}) async-start(bf16[8,8,1]{1,2,0:T(2,128)(2,1)} %all_to_all.52), calls=%async_computation | async-start | bytes 8192 | tf_op jit(solution)/shard_map/all_to_all | solution.py:65
  145.8 20.2 %all-to-all-start.1 = ((bf16[8,8,6144]{2,1,0:T(8,128)(2,1)}), bf16[8,8,6144]{2,1,0:T(8,128)(2,1)S(1)}, u32[]{:S(2)}, u32[]{:S(2)}) async-start(bf16[8,8,6144]{2,1,0:T(8,128)(2,1)} %fusion.5), calls=%async_computation.2 | async-start | bytes 1572864 | tf_op jit(solution)/shard_map/all_to_all | solution.py:64
  166.1 1.8 copy-start.2
  172.4 2.7 copy-start.3
  177.7 2.7 copy-start.4
  177.7 2.7 copy-start.6
  180.4 0.6 copy-start.5
  180.4 0.6 copy-start.7
  184.4 2.7 copy-start.4
  184.4 2.7 copy-start.6
  187.1 0.6 copy-start.5
  187.1 0.6 copy-start.7
  191.1 2.7 copy-start.4
  191.1 2.7 copy-start.6
  193.8 0.6 copy-start.5
  193.8 0.6 copy-start.7
  197.7 2.7 copy-start.4
  197.7 2.7 copy-start.6
  200.4 0.6 copy-start.5
  200.5 0.6 copy-start.7
  204.4 2.7 copy-start.4
  204.4 2.7 copy-start.6
  207.1 0.6 copy-start.5
  207.1 0.6 copy-start.7
  211.1 2.7 copy-start.4
  211.1 2.7 copy-start.6
  213.8 0.6 copy-start.5
  213.8 0.6 copy-start.7
  225.0 11.5 %all-to-all-start.3 = ((f32[8,1,768]{2,1,0:T(1,128)}), f32[8,1,768]{2,1,0:T(1,128)}, u32[]{:S(2)}, u32[]{:S(2)}) async-start(f32[8,1,768]{2,1,0:T(1,128)} %reshape.145), calls=%async_computation.4 | async-start | bytes 49152 | tf_op jit(solution)/shard_map/all_to_all | solution.py:127
  236.6 9.6 %all-to-all-start.4 = ((f32[8,1,768]{2,1,0:T(1,128)}), f32[8,1,768]{2,1,0:T(1,128)}, u32[]{:S(2)}, u32[]{:S(2)}) async-start(f32[8,1,768]{2,1,0:T(1,128)} %reshape.143), calls=%async_computation.5 | async-start | bytes 49152 | tf_op jit(solution)/shard_map/all_to_all | solution.py:128
  246.1 42.0 %all-to-all-start.2 = ((f32[1,1024,768]{2,0,1:T(1,128)}), f32[1,1024,768]{2,0,1:T(1,128)S(1)}, u32[]{:S(2)}, u32[]{:S(2)}) async-start(f32[1,1024,768]{2,0,1:T(1,128)} %copy.112), calls=%async_computation.3 | async-start | bytes 6291456 | tf_op jit(solution)/shard_map/all_to_all | solution.py:124
  288.2 1.9 copy-start
  290.1 1.0 copy-start.8
Sparse Core Ops, SparseCore 0:
  51.4 83.0 reduce-scatter.1
  136.9 29.6 all-gather.1
